TPU v7x, 256 devices: a 8x8x2 block of a 8x8x16 slice. The times are simulated.
256 devices in a mesh: pairs: 2 (over z), band: 128 (over x, y, core).
Axes of the slice: x: 8, y: 8, z: 2, core: 2. Of those that a mesh axis runs over, the one named last changes fastest.
The devices are a block of a 8x8x16 slice.
Arguments:
- query_tiles: bfloat16 [768, 256, 128], P(('pairs', 'band')), parts along dimension 0, may hold values from -52 to 52
- target: bfloat16 [768, 256, 128], P(('pairs', 'band')), parts along dimension 0, may hold values from -6 to 6
- tile_home: int32 [768], P('pairs'), parts along dimension 0, may hold values from 0 to 383, as said below
- candidates: int32 [768, 64], P(('pairs', 'band')), parts along dimension 0, may hold values from 0 to 383, as said below
- valid_mask: int32 [768, 64], P(('pairs', 'band')), parts along dimension 0, may hold values from 0 to 1, as said below
Outputs:
- matched: bfloat16 [768, 256, 128], P(('pairs', 'band')), parts along dimension 0
There are 2 independent parts, one for each index of `pairs`. A program takes and returns all parts, laid end to end along the dimension named above; each array names one. Nothing has to cross between parts.
Inputs may be any that keep to these rules, and one draw needn't show every extreme that they name: `tile_home`: a permutation of 0 to 383; target tile ids that agree modulo 128 are stored on the same device, storage row r lying on device r // 3. Ids in a row are distinct; the candidates of one device's query tiles all lie in one run of 128 consecutive ids taken modulo 384, and its first two query tiles together name every id of that run. `valid_mask`: the first entry of every row is 1.
All inputs are finite; a program needn't handle non-finite values.
Results may differ from a plain program's by a relative error of at most 0.0034.
Values may be sent and summed in bfloat16 or wider, within the bound.
A program may use at most 128 MiB of HBM per device.

v0:
```python
import math

import jax
import jax.numpy as jnp
from jax import lax
from jax.sharding import PartitionSpec as P


def attend_tile(tile_query, tile_keys, keep_mask):
    per_tile = tile_keys.shape[0] // keep_mask.shape[0]
    scores = jnp.dot(tile_query, tile_keys.T, preferred_element_type=jnp.float32) * (
        1.0 / math.sqrt(tile_query.shape[1])
    )
    allowed = jnp.repeat(keep_mask > 0, per_tile)[None, :]
    scores = jnp.where(allowed, scores, -jnp.inf)
    peak = jnp.max(scores, axis=1, keepdims=True)
    raised = jnp.exp(scores - peak)
    totals = jnp.sum(raised, axis=1, keepdims=True)
    weights = (raised / totals).astype(jnp.bfloat16)
    return jnp.dot(weights, tile_keys, preferred_element_type=jnp.float32).astype(jnp.bfloat16)


def body(query_tiles, target, tile_home, candidates, valid_mask):
    channels = target.shape[2]
    stored_rows = tile_home[candidates]
    source = lax.all_gather(target, "band", axis=0, tiled=True)

    def one_tile(packed):
        tile_query, chosen, keep_mask = packed
        stored = source[chosen].reshape(-1, channels)
        return attend_tile(tile_query, stored, keep_mask)

    return lax.map(one_tile, (query_tiles, stored_rows, valid_mask))


def solution(mesh):
    in_specs = (
        P(("pairs", "band"), None, None),
        P(("pairs", "band"), None, None),
        P("pairs"),
        P(("pairs", "band"), None),
        P(("pairs", "band"), None),
    )
    out_specs = P(("pairs", "band"), None, None)
    return jax.shard_map(body, mesh=mesh, in_specs=in_specs, out_specs=out_specs, check_vma=False)
```

profile of v0, /device:TPU:513, one launch (start us, length us, event | category | flops | bytes accessed | tf_op | source)
XLA Modules:
  0.0 268.5 jit_solution(7179833793408976285)
XLA Ops:
  6.6 0.7 all-gather.2.cloned.1.call-update
  7.3 0.7 compare_select_fusion.1
  8.0 0.1 reshape.47
  8.1 1.6 gather_fusion.1
  9.7 0.1 reshape.46
  9.8 136.6 %all-gather.2.cloned.1.call-done = bf16[384,256,128]{2,1,0:T(8,128)(2,1)} async-done(((bf16[3,256,128]{2,1,0:T(8,128)(2,1)}), bf16[384,256,128]{2,1,0:T(8,128)(2,1)}) %all-gather.2.cloned.1.call-update) | async-done | bytes 25165840 | tf_op jit(solution)/shard_map/all_gather | solution.py:26
  146.4 114.5 %while.10 = (s32[]{:T(128)}, bf16[3,256,128]{2,1,0:T(8,128)(2,1)S(1)}, s32[3,64]{1,0:T(4,128)}, bf16[3,256,128]{2,1,0:T(8,128)(2,1)}, s32[3,64]{1,0:T(4,128)S(1)}, /*index=5*/bf16[384,256,128]{2,1,0:T(8,128)(2,1)}, s32[]{:T(128)}) while((s32[]{:T(128)}, bf16[3,256,128]{2,1,0:T(8,128)(2,1)S(1)}, s32[3,64]{1,0:T(4,128)}, ...), condition=%wide.region_3.4_spmd, body=%wide.region_0.3_spmd.sunk | while | flops 2181071616 | bytes 84093936 | solution.py:33
  146.4 11.2 %gather_fusion = bf16[64,256,128]{2,1,0:T(8,128)(2,1)} fusion(bf16[384,256,128]{2,1,0:T(8,128)(2,1)} %get-tuple-element.112, s32[1024]{0:T(1024)S(1)} %pad_clamp_fusion.3), kind=kCustom, calls=%fused_computation.clone.1 | custom fusion | bytes 8388864 | tf_op jit(solution)/shard_map/while/body/eval_jaxpr/gather | solution.py:30
  157.6 0.7 compare_bitcast_fusion.2
  158.4 10.4 %fusion.23 = (f32[256]{0:T(256)S(1)}, f32[256,16384]{1,0:T(8,128)}) fusion(bf16[16384,128]{1,0:T(8,128)(2,1)} %bitcast.38, bf16[3,256,128]{2,1,0:T(8,128)(2,1)} %get-tuple-element.110, s32[]{:T(128)} %get-tuple-element.100, pred[16384]{0:T(1024)(128)(4,1)S(1)} %broadcast_in_dim.37), kind=kOutput, calls=%fused_computation.23.clone.1 | convolution fusion | flops 1086324480 | bytes 21054976 | tf_op jit(solution)/shard_map/while/body/eval_jaxpr/dot_general | solution.py:11
  168.8 8.1 %fusion.24 = f32[256]{0:T(256)S(1)} fusion(f32[256,16384]{1,0:T(8,128)} %get-tuple-element.91, f32[256]{0:T(256)S(1)} %get-tuple-element.92), kind=kLoop, calls=%fused_computation.6.clone.1 | loop fusion | flops 8388352 | bytes 16779264 | tf_op jit(solution)/shard_map/while/body/eval_jaxpr/reduce_sum | solution.py:18
  177.0 7.6 %fusion.25 = bf16[3,256,128]{2,1,0:T(8,128)(2,1)S(1)} fusion(bf16[3,256,128]{2,1,0:T(8,128)(2,1)S(1)} %get-tuple-element.101, s32[]{:T(128)} %get-tuple-element.100, bf16[16384,128]{1,0:T(8,128)(2,1)S(1)} %bitcast.39, f32[256,16384]{1,0:T(8,128)} %get-tuple-element.91, f32[256]{0:T(256)S(1)} %fusion.24, f32[256]{0:T(256)S(1)} %get-tuple-element.92), kind=kOutput, calls=%fused_computation.10.clone.1 | convolution fusion | flops 1086357504 | bytes 21039108 | tf_op jit(solution)/shard_map/while/body/eval_jaxpr/dot_general | solution.py:20
  184.6 11.2 %gather_fusion = bf16[64,256,128]{2,1,0:T(8,128)(2,1)} fusion(bf16[384,256,128]{2,1,0:T(8,128)(2,1)} %get-tuple-element.112, s32[1024]{0:T(1024)S(1)} %pad_clamp_fusion.3), kind=kCustom, calls=%fused_computation.clone.1 | custom fusion | bytes 8388864 | tf_op jit(solution)/shard_map/while/body/eval_jaxpr/gather | solution.py:30
  195.8 0.7 compare_bitcast_fusion.2
  196.4 0.1 broadcast_in_dim.36
  196.6 10.4 %fusion.23 = (f32[256]{0:T(256)S(1)}, f32[256,16384]{1,0:T(8,128)}) fusion(bf16[16384,128]{1,0:T(8,128)(2,1)} %bitcast.38, bf16[3,256,128]{2,1,0:T(8,128)(2,1)} %get-tuple-element.110, s32[]{:T(128)} %get-tuple-element.100, pred[16384]{0:T(1024)(128)(4,1)S(1)} %broadcast_in_dim.37), kind=kOutput, calls=%fused_computation.23.clone.1 | convolution fusion | flops 1086324480 | bytes 21054976 | tf_op jit(solution)/shard_map/while/body/eval_jaxpr/dot_general | solution.py:11
  207.0 8.1 %fusion.24 = f32[256]{0:T(256)S(1)} fusion(f32[256,16384]{1,0:T(8,128)} %get-tuple-element.91, f32[256]{0:T(256)S(1)} %get-tuple-element.92), kind=kLoop, calls=%fused_computation.6.clone.1 | loop fusion | flops 8388352 | bytes 16779264 | tf_op jit(solution)/shard_map/while/body/eval_jaxpr/reduce_sum | solution.py:18
  215.1 7.6 %fusion.25 = bf16[3,256,128]{2,1,0:T(8,128)(2,1)S(1)} fusion(bf16[3,256,128]{2,1,0:T(8,128)(2,1)S(1)} %get-tuple-element.101, s32[]{:T(128)} %get-tuple-element.100, bf16[16384,128]{1,0:T(8,128)(2,1)S(1)} %bitcast.39, f32[256,16384]{1,0:T(8,128)} %get-tuple-element.91, f32[256]{0:T(256)S(1)} %fusion.24, f32[256]{0:T(256)S(1)} %get-tuple-element.92), kind=kOutput, calls=%fused_computation.10.clone.1 | convolution fusion | flops 1086357504 | bytes 21039108 | tf_op jit(solution)/shard_map/while/body/eval_jaxpr/dot_general | solution.py:20
  222.8 11.2 %gather_fusion = bf16[64,256,128]{2,1,0:T(8,128)(2,1)} fusion(bf16[384,256,128]{2,1,0:T(8,128)(2,1)} %get-tuple-element.112, s32[1024]{0:T(1024)S(1)} %pad_clamp_fusion.3), kind=kCustom, calls=%fused_computation.clone.1 | custom fusion | bytes 8388864 | tf_op jit(solution)/shard_map/while/body/eval_jaxpr/gather | solution.py:30
  234.0 0.7 compare_bitcast_fusion.2
  234.8 10.4 %fusion.23 = (f32[256]{0:T(256)S(1)}, f32[256,16384]{1,0:T(8,128)}) fusion(bf16[16384,128]{1,0:T(8,128)(2,1)} %bitcast.38, bf16[3,256,128]{2,1,0:T(8,128)(2,1)} %get-tuple-element.110, s32[]{:T(128)} %get-tuple-element.100, pred[16384]{0:T(1024)(128)(4,1)S(1)} %broadcast_in_dim.37), kind=kOutput, calls=%fused_computation.23.clone.1 | convolution fusion | flops 1086324480 | bytes 21054976 | tf_op jit(solution)/shard_map/while/body/eval_jaxpr/dot_general | solution.py:11
  245.2 8.1 %fusion.24 = f32[256]{0:T(256)S(1)} fusion(f32[256,16384]{1,0:T(8,128)} %get-tuple-element.91, f32[256]{0:T(256)S(1)} %get-tuple-element.92), kind=kLoop, calls=%fused_computation.6.clone.1 | loop fusion | flops 8388352 | bytes 16779264 | tf_op jit(solution)/shard_map/while/body/eval_jaxpr/reduce_sum | solution.py:18
  253.3 7.6 %fusion.25 = bf16[3,256,128]{2,1,0:T(8,128)(2,1)S(1)} fusion(bf16[3,256,128]{2,1,0:T(8,128)(2,1)S(1)} %get-tuple-element.101, s32[]{:T(128)} %get-tuple-element.100, bf16[16384,128]{1,0:T(8,128)(2,1)S(1)} %bitcast.39, f32[256,16384]{1,0:T(8,128)} %get-tuple-element.91, f32[256]{0:T(256)S(1)} %fusion.24, f32[256]{0:T(256)S(1)} %get-tuple-element.92), kind=kOutput, calls=%fused_computation.10.clone.1 | convolution fusion | flops 1086357504 | bytes 21039108 | tf_op jit(solution)/shard_map/while/body/eval_jaxpr/dot_general | solution.py:20
  261.0 0.7 copy-done.2
  (23 shorter events, 0.3 us)
Async XLA Ops:
  6.5 1.6 copy-start
  6.6 139.9 %all-gather.2.cloned.1.call-start = ((), (), s32[]{:S(2)}) async-start(), calls=%async_computation | async-start | bytes 25362432 | tf_op jit(solution)/shard_map/all_gather | solution.py:26
  158.4 18.6 %copy-start.1 = (bf16[64,256,128]{2,1,0:T(8,128)(2,1)S(1)}, bf16[64,256,128]{2,1,0:T(8,128)(2,1)}, u32[]{:S(2)}) copy-start(bf16[64,256,128]{2,1,0:T(8,128)(2,1)} %gather_fusion) | copy-start | bytes 12582916 | tf_op jit(solution)/shard_map/while
  196.6 18.6 %copy-start.1 = (bf16[64,256,128]{2,1,0:T(8,128)(2,1)S(1)}, bf16[64,256,128]{2,1,0:T(8,128)(2,1)}, u32[]{:S(2)}) copy-start(bf16[64,256,128]{2,1,0:T(8,128)(2,1)} %gather_fusion) | copy-start | bytes 12582916 | tf_op jit(solution)/shard_map/while
  234.7 18.6 %copy-start.1 = (bf16[64,256,128]{2,1,0:T(8,128)(2,1)S(1)}, bf16[64,256,128]{2,1,0:T(8,128)(2,1)}, u32[]{:S(2)}) copy-start(bf16[64,256,128]{2,1,0:T(8,128)(2,1)} %gather_fusion) | copy-start | bytes 12582916 | tf_op jit(solution)/shard_map/while
  261.0 0.7 copy-start.2
Sparse Core Ops, SparseCore 0:
  9.9 136.4 all-gather.1
where the time goes:
time: 269 us; the launch traced here: 268 us
  waiting for transfers between devices  137 us (51%)
  matrix products  54.1 us (20%)
  local copies, waits for them, and re-layouts  36.2 us (13%)
  other arithmetic  27.2 us (10%)
  between operations  13.4 us (5%)
    all_gather x1, waiting for transfers between devices, body(): source = lax.all_gather(target, 'band', axis=0, tiled=True)  137 us
    gather x3, local copies, waits for them, and re-layouts, one_tile(): stored = source[chosen].reshape(-1, channels)  33.5 us
    dot_general x3, matrix products, attend_tile(): jnp.dot(tile_query, tile_keys.T, preferred_element_type=jnp.float32)  31.3 us
    reduce_sum x3, other arithmetic, attend_tile(): totals = jnp.sum(raised, axis=1, keepdims=True)  24.4 us
    dot_general x3, matrix products, attend_tile(): jnp.dot(weights, tile_keys, preferred_element_type=jnp.float32)  22.8 us
  transfers between devices with their start and end apart: 1, of which 1 were waited for; matrix products, arithmetic and copies ran while one was open for 1% of the time, Pallas kernels for 0%

commit v1 on v0

v1 whole, which is shorter than its diff:
```python
import functools
import math

import jax
import jax.numpy as jnp
from jax import lax
from jax.experimental import pallas as pl
from jax.experimental.pallas import tpu as pltpu
from jax.sharding import PartitionSpec as P

NEG = -1e30
MESH = pl.DeviceIdType.MESH
HEAD = (0, -3, 3)
LEAF_B = (-3, 3, 2, -2, 4)
LEAF_A = (0, -1, 1)
LEAF_G = (0, -1, -2, -3, 1, 2, 3, 4)


def ring_slot(way, hop):
    return 3 * way + hop - 1 if hop <= 3 else 6


def row_offset(k):
    return -(k + 1) if k < 3 else (k - 2 if k < 6 else 4)


def kernel(side, bias_ref, sel_ref, q_ref, own_ref, out_ref, *scratch):
    (spine, row, st_a, st_b1u, st_b1d, st_b2u, st_b2d, st_p, kfa, kfb, kfg, tabv, tabs, qt, acc, mx, tot,
     s_spine, r_spine, s_row, r_row, s_a, s_b1u, s_b1d, s_b2u, s_b2d, s_p, r_a, r_b, r_g, s_tab, r_tab, l_tab) = scratch
    n_q, rows_q, channels = q_ref.shape
    half = rows_q // 2
    scale = math.log2(math.e) / math.sqrt(channels)
    me = lax.axis_index("band")
    core = lax.rem(me, 2)
    chip = lax.div(me, 2)
    x, y = lax.div(chip, side), lax.rem(chip, side)
    mine = (1 - core) * x + core * y, (1 - core) * y + core * x

    def place(net, at, dr, ds):
        r, s = lax.rem(at[0] + dr + side, side), lax.rem(at[1] + ds + side, side)
        xx, yy = (1 - net) * r + net * s, (1 - net) * s + net * r
        return (xx * side + yy) * 2

    def dev(dr, ds, other=False):
        return {"band": place(core, mine, dr, ds) + (1 - core if other else core)}

    def source(net, dr, ds):
        if net == 0:
            return place(core, mine, dr, ds) + core
        return place(1 - core, (mine[1], mine[0]), dr, ds) + (1 - core)

    partner = dev(0, 0, True)

    def send(src, dst, ssem, rsem, to):
        pltpu.make_async_remote_copy(
            src_ref=src, dst_ref=dst, send_sem=ssem, recv_sem=rsem, device_id=to, device_id_type=MESH
        ).start()

    def take(ref, sem):
        pltpu.make_async_remote_copy(
            src_ref=ref, dst_ref=ref, send_sem=sem, recv_sem=sem, device_id=partner, device_id_type=MESH
        ).wait_recv()

    def drain(ref, sem):
        pltpu.make_async_remote_copy(
            src_ref=ref, dst_ref=ref, send_sem=sem, recv_sem=sem, device_id=partner, device_id_type=MESH
        ).wait_send()

    barrier = pltpu.get_barrier_semaphore()
    greeted = [partner]
    for d in (-1, 1):
        for other in (False, True):
            greeted += [dev(d, 0, other), dev(0, d, other)]
    for to in greeted:
        pl.semaphore_signal(barrier, inc=1, device_id=to, device_id_type=MESH)
    pl.semaphore_wait(barrier, len(greeted))

    def head(j):
        return own_ref if j == 0 else spine.at[j - 1, 2]

    def spine_send(way, hop, t):
        src = own_ref.at[t] if hop == 1 else spine.at[way, hop - 2, t]
        send(src, spine.at[way, hop - 1, t], s_spine, r_spine.at[way, hop - 1, t], dev(0, 1 - 2 * way))

    def row_send(j, way, hop, t):
        src = head(j).at[t] if hop == 1 else row.at[j, ring_slot(way, hop - 1), t]
        dst = row.at[j, ring_slot(way, hop), t]
        sem = r_row.at[j, ring_slot(way, hop), t]
        if hop == 4:
            part = pl.ds(way * half, half)
            src, dst, sem = src.at[part], dst.at[part], r_row.at[j, 6 + way, t]
        send(src, dst, s_row.at[j], sem, dev(1 - 2 * way, 0))

    def row_take(j, way, hop, t):
        ref = row.at[j, ring_slot(way, hop), t]
        if hop == 4:
            take(ref.at[pl.ds(way * half, half)], r_row.at[j, 6 + way, t])
        else:
            take(ref, r_row.at[j, ring_slot(way, hop), t])

    send(sel_ref, tabv.at[0], s_tab, r_tab, dev(0, -1))
    send(sel_ref, tabv.at[1], s_tab, r_tab, dev(0, 1))
    send(sel_ref, tabv.at[2], s_tab, r_tab, dev(-1, 0, True))
    send(sel_ref, tabv.at[3], s_tab, r_tab, dev(1, 0, True))
    send(sel_ref, tabv.at[4], s_tab, r_tab, partner)
    for t in range(3):
        for way in range(2):
            spine_send(way, 1, t)
            row_send(0, way, 1, t)
    own_tab = pltpu.make_async_copy(sel_ref, tabs.at[5], l_tab.at[0])
    own_tab.start()

    for q in range(n_q):
        qt[:, pl.ds(q * rows_q, rows_q)] = q_ref[q].T
    acc[...] = jnp.zeros_like(acc)
    tot[...] = jnp.zeros_like(tot)
    mx[...] = jnp.full_like(mx, NEG)

    own_tab.wait()
    take(tabv, r_tab)
    got = pltpu.make_async_copy(tabv, tabs.at[pl.ds(0, 5)], l_tab.at[1])
    got.start()
    got.wait()

    def pack(src, who, outs):
        step = 64
        for lo in range(0, rows_q, step):
            tiles = [src[t, pl.ds(lo, step), :] for t in range(3)]
            for table, dst, first, count in outs:
                if first <= lo < first + count:
                    which = tabs[table, 0, who]
                    dst[pl.ds(lo - first, step), :] = jnp.where(
                        which == 0, tiles[0], jnp.where(which == 1, tiles[1], tiles[2])
                    )

    up = (dev(0, 1), dev(0, 1, True))
    down = (dev(0, -1), dev(0, -1, True))
    whole = (0, rows_q)
    low, high = (0, half), (half, half)

    def pack_trunk(src, who, place_self, index_p, place_p, sem_p, more):
        outs = [(5, place_self, *whole), (4, st_p.at[index_p], *whole)]
        outs += [(table, stage, *rng) for table, stage, rng, *_ in more]
        pack(src, who, outs)
        for _, stage, _, dst, ssem, rsem, to in more:
            send(stage, dst, ssem, rsem, to)
        send(st_p.at[index_p], place_p, s_p, sem_p, partner)

    def pack_row(j, k):
        who = source(0, row_offset(k), HEAD[j])
        more = []
        for o in range(2):
            t_up, t_dn = 2 * o, 2 * o + 1
            if j == 0:
                more.append((t_up, st_a.at[k, o], whole, kfa.at[o, k, 1], s_a, r_a.at[o, k], up[o]))
                more.append((t_dn, st_a.at[k, 2 + o], whole, kfa.at[o, k, 2], s_a, r_a.at[o, k], down[o]))
            elif j == 1:
                more.append((t_dn, st_b1d.at[k, o], whole, kfb.at[o, k, 3], s_b1d, r_b.at[o, k], down[o]))
                more.append((t_up, st_b1u.at[k, o], low, kfb.at[o, k, 4, pl.ds(0, half)], s_b1u, r_b.at[o, k], up[o]))
            else:
                more.append((t_up, st_b2u.at[k, o], whole, kfb.at[o, k, 2], s_b2u, r_b.at[o, k], up[o]))
                more.append((t_dn, st_b2d.at[k, o], high, kfb.at[o, k, 4, pl.ds(half, half)], s_b2d, r_b.at[o, k], down[o]))
        if j == 0:
            pack_trunk(row.at[j, k], who, kfa.at[0, k, 0], 7 + k, kfa.at[1, k, 0], r_a.at[1, k], more)
        else:
            pack_trunk(row.at[j, k], who, kfb.at[0, k, j - 1], 7 + 7 * j + k, kfb.at[1, k, j - 1], r_b.at[1, k], more)

    def pack_spine(way, hop):
        slot = 3 * way + hop
        more = []
        if hop == 3:
            for o in range(2):
                if way == 0:
                    more.append((2 * o, st_b1u.at[7, o], low, kfg.at[o, 7, pl.ds(0, half)], s_b1u, r_g.at[o], up[o]))
                else:
                    more.append((2 * o + 1, st_b2d.at[7, o], high, kfg.at[o, 7, pl.ds(half, half)], s_b2d, r_g.at[o], down[o]))
        pack_trunk(spine.at[way, hop - 1], source(0, 0, LEAF_G[slot]), kfg.at[0, slot], slot, kfg.at[1, slot], r_g.at[1], more)

    pack_trunk(own_ref, me, kfg.at[0, 0], 0, kfg.at[1, 0], r_g.at[1], [])

    for hop in range(1, 4):
        for t in range(3):
            for way in range(2):
                take(spine.at[way, hop - 1, t], r_spine.at[way, hop - 1, t])
                if hop < 3:
                    spine_send(way, hop + 1, t)
                else:
                    for w in range(2):
                        row_send(1 + way, w, 1, t)
        for t in range(3):
            for way in range(2):
                row_take(0, way, hop, t)
                row_send(0, way, hop + 1, t)
        for way in range(2):
            pack_row(0, ring_slot(way, hop))
            pack_spine(way, hop)
    for t in range(3):
        for way in range(2):
            row_take(0, way, 4, t)
    pack_row(0, 6)
    for hop in range(1, 5):
        for j in (1, 2):
            for t in range(3):
                for way in range(2):
                    row_take(j, way, hop, t)
                    if hop < 4:
                        row_send(j, way, hop + 1, t)
            for way in range(2 if hop < 4 else 1):
                pack_row(j, ring_slot(way, hop))

    def attend(ref, whos):
        count = len(whos)
        keys = ref[...].reshape(count * rows_q, channels)
        keys_t = keys.T
        for q in range(n_q):
            cols = pl.ds(q * rows_q, rows_q)
            s = jnp.dot(keys, qt[:, cols], preferred_element_type=jnp.float32)
            parts = [s[t * rows_q:(t + 1) * rows_q] for t in range(count)]
            bias = [bias_ref[q, who] for who in whos]
            tops = [jnp.max(p, axis=0, keepdims=True) * scale for p in parts]
            before = mx[q]
            now = before
            for t in range(count):
                now = jnp.maximum(now, tops[t] + bias[t])
            alpha = jnp.exp2(before - now)
            total = alpha * tot[q]
            ps = []
            for t in range(count):
                p = jnp.exp2(parts[t] * scale - jnp.maximum(now - bias[t], tops[t]))
                total = total + jnp.sum(p, axis=0, keepdims=True)
                ps.append(p.astype(jnp.bfloat16))
            mx[q] = now
            tot[q] = total
            pv = jnp.dot(keys_t, jnp.concatenate(ps, axis=0), preferred_element_type=jnp.float32)
            acc[:, cols] = acc[:, cols] * alpha + pv

    def dyn_offset(k):
        return jnp.where(k < 3, -(k + 1), jnp.where(k < 6, k - 2, 4))

    for net in range(2):
        take(kfg.at[0, 7] if net == 0 else kfg.at[1], r_g.at[net])

        def unit_g(h, _):
            offs = [jnp.where(h == 0, LEAF_G[t], LEAF_G[4 + t]) for t in range(4)]
            attend(kfg.at[net, pl.ds(4 * h, 4)], [source(net, 0, o) for o in offs])
            return 0

        lax.fori_loop(0, 2, unit_g, 0)

        def unit_a(k, _):
            take(kfa.at[0, k, pl.ds(1, 2)] if net == 0 else kfa.at[1, k], r_a.at[net, k])
            attend(kfa.at[net, k], [source(net, dyn_offset(k), o) for o in LEAF_A])
            return 0

        lax.fori_loop(0, 7, unit_a, 0)

    for net in range(2):
        def unit_b(k, _):
            take(kfb.at[0, k, pl.ds(2, 3)] if net == 0 else kfb.at[1, k], r_b.at[net, k])
            attend(kfb.at[net, k], [source(net, dyn_offset(k), o) for o in LEAF_B])
            return 0

        lax.fori_loop(0, 7, unit_b, 0)

    for q in range(n_q):
        out_ref[q] = (acc[:, pl.ds(q * rows_q, rows_q)] / tot[q]).T.astype(out_ref.dtype)

    drain(spine, s_spine)
    for j in range(3):
        drain(row.at[j], s_row.at[j])
    drain(st_a, s_a)
    drain(st_b1u, s_b1u)
    drain(st_b1d, s_b1d)
    drain(st_b2u, s_b2u)
    drain(st_b2d, s_b2d)
    drain(st_p, s_p)
    drain(tabv, s_tab)


def body(side, query_tiles, target, tile_home, candidates, valid_mask):
    n_band = 2 * side * side
    tiles_dev, rows_q, channels = target.shape
    half = rows_q // 2
    ids = lax.broadcasted_iota(jnp.int32, (1, 1, tile_home.shape[0]), 2)
    stored = jnp.sum(jnp.where(candidates[:, :, None] == ids, tile_home[None, None, :], 0), axis=2)
    hit = (stored // tiles_dev)[:, :, None] == lax.broadcasted_iota(jnp.int32, (1, 1, n_band), 2)
    sel = jnp.sum(jnp.where(hit[:2], (stored % tiles_dev)[:2, :, None], 0), axis=(0, 1))
    sel = jnp.broadcast_to(sel[None, :], (8, n_band))
    used = jnp.any(hit & (valid_mask > 0)[:, :, None], axis=1)
    bias = jnp.where(used, 0.0, NEG).astype(jnp.float32)

    def tile(*lead):
        return pltpu.VMEM((*lead, rows_q, channels), target.dtype)

    def halves(*lead):
        return pltpu.VMEM((*lead, half, channels), target.dtype)

    dma = pltpu.SemaphoreType.DMA
    n_q = query_tiles.shape[0]
    scratch = [
        tile(2, 3, 3), tile(3, 7, 3), tile(7, 4), halves(8, 2), tile(7, 2), tile(7, 2), halves(8, 2), tile(28),
        tile(2, 7, 3), tile(2, 7, 5), tile(2, 8),
        pltpu.VMEM((5, 8, n_band), jnp.int32), pltpu.SMEM((6, 8, n_band), jnp.int32),
        pltpu.VMEM((channels, n_q * rows_q), target.dtype),
        pltpu.VMEM((channels, n_q * rows_q), jnp.float32),
        pltpu.VMEM((n_q, 1, rows_q), jnp.float32), pltpu.VMEM((n_q, 1, rows_q), jnp.float32),
        dma, dma((2, 3, 3)), dma((3,)), dma((3, 8, 3)), dma, dma, dma, dma, dma, dma,
        dma((2, 7)), dma((2, 7)), dma((2,)), dma, dma, dma((2,)),
    ]
    vmem = pl.BlockSpec(memory_space=pltpu.VMEM)
    return pl.pallas_call(
        functools.partial(kernel, side),
        out_shape=jax.ShapeDtypeStruct(query_tiles.shape, query_tiles.dtype),
        in_specs=[pl.BlockSpec(memory_space=pltpu.SMEM), vmem, vmem, vmem],
        out_specs=vmem,
        scratch_shapes=scratch,
        compiler_params=pltpu.CompilerParams(
            collective_id=0, has_side_effects=True, vmem_limit_bytes=60 * 1024 * 1024
        ),
    )(bias, sel, query_tiles, target)


def solution(mesh):
    side = math.isqrt(mesh.shape["band"] // 2)
    in_specs = (
        P(("pairs", "band"), None, None),
        P(("pairs", "band"), None, None),
        P("pairs"),
        P(("pairs", "band"), None),
        P(("pairs", "band"), None),
    )
    out_specs = P(("pairs", "band"), None, None)
    return jax.shard_map(
        functools.partial(body, side), mesh=mesh, in_specs=in_specs, out_specs=out_specs, check_vma=False
    )
```

time: 269 us -> 155 us (0.58)
  Pallas kernels: 0 us -> 149 us
  waiting for transfers between devices: 137 us -> 0 us
  matrix products: 54.1 us -> 0 us
  local copies, waits for them, and re-layouts: 36.2 us -> 2.22 us
  other arithmetic: 27.2 us -> 2.43 us
  between operations: 13.4 us -> 0.02 us
    pallas_call x0 -> x1, Pallas kernels: none -> 149 us  [body(): pl.pallas_call(functools.partial(kernel, side), out_shape=jax.ShapeDtypeS...]
    all_gather x1 -> x0, waiting for transfers between devices: 137 us -> none  [body(): source = lax.all_gather(target, 'band', axis=0, tiled=True)]
    dot_general x6 -> x0, matrix products: 54.1 us -> none  [the longest x3 31.3 us: attend_tile(): jnp.dot(tile_query, tile_keys.T, preferred_element_type=jnp.float32)]
    gather x5 -> x0, local copies, waits for them, and re-layouts: 35.2 us -> none  [the longest x3 33.5 us: one_tile(): stored = source[chosen].reshape(-1, channels)]
    reduce_sum x3 -> x2, other arithmetic: 24.4 us -> 1 us  [the longest x1 0.9 us: body(): jnp.sum(jnp.where(candidates[:, :, None] == ids, tile_home[None, None, :]...]
  transfers between devices with their start and end apart: 1 -> 0, of which waited for: 1 -> 0; matrix products, arithmetic and copies ran while one was open for 1% -> 0% of each run, Pallas kernels for 0% -> 0%
where the time goes in v1:
time: 155 us; the launch traced here: 154 us
  Pallas kernels  149 us (96%)
  other arithmetic  2.43 us (2%)
  local copies, waits for them, and re-layouts  2.22 us (1%)
    pallas_call x1, Pallas kernels, body(): pl.pallas_call(functools.partial(kernel, side), out_shape=jax.ShapeDtypeS...  149 us

profile of v1, /device:TPU:513, one launch (start us, length us, event | category | flops | bytes accessed | tf_op | source)
XLA Modules:
  0.0 153.8 jit_solution(10678362227468483921)
XLA Ops:
  0.0 0.0 copy-start
  0.0 0.7 broadcast_compare_fusion
  0.7 0.0 copy-done
  0.7 0.9 select_reduce_fusion
  1.6 0.1 iota_compare_fusion.1
  1.8 0.1 select_reduce_fusion.1
  1.9 0.6 broadcast_select_fusion.bias_ref
  2.5 0.6 broadcast_in_dim.49.sel_ref
  3.0 149.1 %shard_map.55 = bf16[3,256,128]{2,1,0:T(8,128)(2,1)} custom-call(f32[3,128]{1,0:T(4,128)} %broadcast_select_fusion.bias_ref, s32[8,128]{1,0:T(8,128)} %broadcast_in_dim.49.sel_ref, bf16[3,256,128]{2,1,0:T(8,128)(2,1)} %q_ref.1, bf16[3,256,128]{2,1,0:T(8,128)(2,1)} %own_ref.1), custom_call_target="tpu_custom_call" | custom-call | tf_op jit(solution)/shard_map/pallas_call | solution.py:311
  152.2 1.6 %copy.7 = bf16[3,256,128]{2,1,0:T(8,128)(2,1)} copy(bf16[3,256,128]{2,1,0:T(8,128)(2,1)} %shard_map.55) | data formatting | bytes 393216
  (2 shorter events, 0.0 us)
Async XLA Ops:
  0.0 0.7 copy-start

commit v2 on v1

--- a/solution.py
+++ b/solution.py
@@ -25,8 +25,8 @@
 
 
 def kernel(side, bias_ref, sel_ref, q_ref, own_ref, out_ref, *scratch):
-    (spine, row, st_a, st_b1u, st_b1d, st_b2u, st_b2d, st_p, kfa, kfb, kfg, tabv, tabs, qt, acc, mx, tot,
-     s_spine, r_spine, s_row, r_row, s_a, s_b1u, s_b1d, s_b2u, s_b2d, s_p, r_a, r_b, r_g, s_tab, r_tab, l_tab) = scratch
+    (spine, row, st_a, st_b1u, st_b1d, st_b2u, st_b2d, st_p, kfa, kfb, kfg, tabv, tabs, qt, acc, mx, ktb,
+     sc0, sc1, sc2, pr0, pr1, pr2, tp0, tp1, tp2, s_spine, r_spine, s_row, r_row, s_a, s_b1u, s_b1d, s_b2u, s_b2d, s_p, r_a, r_b, r_g, s_tab, r_tab, l_tab) = scratch
     n_q, rows_q, channels = q_ref.shape
     half = rows_q // 2
     scale = math.log2(math.e) / math.sqrt(channels)
@@ -45,9 +45,8 @@
         return {"band": place(core, mine, dr, ds) + (1 - core if other else core)}
 
     def source(net, dr, ds):
-        if net == 0:
-            return place(core, mine, dr, ds) + core
-        return place(1 - core, (mine[1], mine[0]), dr, ds) + (1 - core)
+        n = core * (1 - net) + (1 - core) * net
+        return place(n, ((1 - n) * x + n * y, (1 - n) * y + n * x), dr, ds) + n
 
     partner = dev(0, 0, True)
 
@@ -111,10 +110,13 @@
     own_tab.start()
 
     for q in range(n_q):
-        qt[:, pl.ds(q * rows_q, rows_q)] = q_ref[q].T
+        scaled = q_ref[q].astype(jnp.float32).T * scale
+        hi = scaled.astype(qt.dtype)
+        qt[q, pl.ds(0, channels), :] = hi
+        qt[q, pl.ds(channels, channels), :] = (scaled - hi.astype(jnp.float32)).astype(qt.dtype)
     acc[...] = jnp.zeros_like(acc)
-    tot[...] = jnp.zeros_like(tot)
     mx[...] = jnp.full_like(mx, NEG)
+    ktb[pl.ds(channels, 16), :] = jnp.ones((16, ktb.shape[1]), ktb.dtype)
 
     own_tab.wait()
     take(tabv, r_tab)
@@ -177,6 +179,89 @@
         pack_trunk(spine.at[way, hop - 1], source(0, 0, LEAF_G[slot]), kfg.at[0, slot], slot, kfg.at[1, slot], r_g.at[1], more)
 
     pack_trunk(own_ref, me, kfg.at[0, 0], 0, kfg.at[1, 0], r_g.at[1], [])
+
+    scores, probs, tops = (sc0, sc1, sc2), (pr0, pr1, pr2), (tp0, tp1, tp2)
+
+    def attend(units, width, ref_of, whos_of):
+        keys = width * rows_q
+
+        def score(q, ref):
+            for t in range(width):
+                k = ref[t]
+                s = jnp.dot(jnp.concatenate([k, k], axis=1), qt[q], preferred_element_type=jnp.float32)
+                scores[q][pl.ds(t * rows_q, rows_q), :] = s
+                tops[q][t] = jnp.max(s, axis=0, keepdims=True)
+
+        def soften(q, bias):
+            before = mx[q]
+            now = before
+            top = [tops[q][t] for t in range(width)]
+            for t in range(width):
+                now = jnp.maximum(now, top[t] + bias[t])
+            for t in range(width):
+                rows = pl.ds(t * rows_q, rows_q)
+                shift = jnp.maximum(now - bias[t], top[t])
+                probs[q][rows, :] = jnp.exp2(scores[q][rows, :] - shift).astype(jnp.bfloat16)
+            mx[q] = now
+            return jnp.exp2(before - now)
+
+        def mix(q, alpha):
+            pv = jnp.dot(ktb[:, pl.ds(0, keys)], probs[q][pl.ds(0, keys), :], preferred_element_type=jnp.float32)
+            acc[q] = acc[q] * alpha + pv
+
+        def unit(u, _):
+            ref = ref_of(u)
+            following = ref_of(jnp.minimum(u + 1, units - 1))
+            whos = whos_of(u)
+            ktb[pl.ds(0, channels), pl.ds(0, keys)] = ref[...].reshape(keys, channels).T
+            alphas = []
+            for q in range(n_q):
+                score((q + 1) % n_q, ref if q + 1 < n_q else following)
+                alphas.append(soften(q, [bias_ref[q, who] for who in whos]))
+                if q > 0:
+                    mix(q - 1, alphas[q - 1])
+            mix(n_q - 1, alphas[n_q - 1])
+            return 0
+
+        score(0, ref_of(0))
+        lax.fori_loop(0, units, unit, 0)
+
+    def attend_g():
+        take(kfg.at[0, 7], r_g.at[0])
+        take(kfg.at[1], r_g.at[1])
+
+        def whos(u):
+            offs = [jnp.where(lax.rem(u, 2) == 0, LEAF_G[t], LEAF_G[4 + t]) for t in range(4)]
+            return [source(lax.div(u, 2), 0, o) for o in offs]
+
+        attend(4, 4, lambda u: kfg.at[lax.div(u, 2), pl.ds(4 * lax.rem(u, 2), 4)], whos)
+
+    def attend_row(hop, ref, sem, skip, offs):
+        ways = 2 if hop < 4 else 1
+        for way in range(ways):
+            k = ring_slot(way, hop)
+            take(ref.at[0, k, pl.ds(skip, ref.shape[2] - skip)], sem.at[0, k])
+            take(ref.at[1, k], sem.at[1, k])
+
+        def at(u):
+            return lax.div(u, ways), lax.rem(u, ways)
+
+        def unit_ref(u):
+            net, way = at(u)
+            return ref.at[net, 3 * way + hop - 1 if hop < 4 else 6]
+
+        def whos(u):
+            net, way = at(u)
+            dr = hop * (2 * way - 1) if hop < 4 else 4
+            return [source(net, dr, o) for o in offs]
+
+        attend(2 * ways, len(offs), unit_ref, whos)
+
+    def attend_a(hop):
+        attend_row(hop, kfa, r_a, 1, LEAF_A)
+
+    def attend_b(hop):
+        attend_row(hop, kfb, r_b, 2, LEAF_B)
 
     for hop in range(1, 4):
         for t in range(3):
@@ -198,6 +283,12 @@
         for way in range(2):
             row_take(0, way, 4, t)
     pack_row(0, 6)
+    covers = {
+        (1, 1): [attend_g], (1, 2): [lambda: attend_a(1)],
+        (2, 1): [lambda: attend_a(2)], (2, 2): [lambda: attend_a(3)],
+        (3, 1): [lambda: attend_a(4)], (3, 2): [lambda: attend_b(1)],
+        (4, 1): [], (4, 2): [lambda: attend_b(2), lambda: attend_b(3), lambda: attend_b(4)],
+    }
     for hop in range(1, 5):
         for j in (1, 2):
             for t in range(3):
@@ -207,63 +298,11 @@
                         row_send(j, way, hop + 1, t)
             for way in range(2 if hop < 4 else 1):
                 pack_row(j, ring_slot(way, hop))
-
-    def attend(ref, whos):
-        count = len(whos)
-        keys = ref[...].reshape(count * rows_q, channels)
-        keys_t = keys.T
-        for q in range(n_q):
-            cols = pl.ds(q * rows_q, rows_q)
-            s = jnp.dot(keys, qt[:, cols], preferred_element_type=jnp.float32)
-            parts = [s[t * rows_q:(t + 1) * rows_q] for t in range(count)]
-            bias = [bias_ref[q, who] for who in whos]
-            tops = [jnp.max(p, axis=0, keepdims=True) * scale for p in parts]
-            before = mx[q]
-            now = before
-            for t in range(count):
-                now = jnp.maximum(now, tops[t] + bias[t])
-            alpha = jnp.exp2(before - now)
-            total = alpha * tot[q]
-            ps = []
-            for t in range(count):
-                p = jnp.exp2(parts[t] * scale - jnp.maximum(now - bias[t], tops[t]))
-                total = total + jnp.sum(p, axis=0, keepdims=True)
-                ps.append(p.astype(jnp.bfloat16))
-            mx[q] = now
-            tot[q] = total
-            pv = jnp.dot(keys_t, jnp.concatenate(ps, axis=0), preferred_element_type=jnp.float32)
-            acc[:, cols] = acc[:, cols] * alpha + pv
-
-    def dyn_offset(k):
-        return jnp.where(k < 3, -(k + 1), jnp.where(k < 6, k - 2, 4))
-
-    for net in range(2):
-        take(kfg.at[0, 7] if net == 0 else kfg.at[1], r_g.at[net])
-
-        def unit_g(h, _):
-            offs = [jnp.where(h == 0, LEAF_G[t], LEAF_G[4 + t]) for t in range(4)]
-            attend(kfg.at[net, pl.ds(4 * h, 4)], [source(net, 0, o) for o in offs])
-            return 0
-
-        lax.fori_loop(0, 2, unit_g, 0)
-
-        def unit_a(k, _):
-            take(kfa.at[0, k, pl.ds(1, 2)] if net == 0 else kfa.at[1, k], r_a.at[net, k])
-            attend(kfa.at[net, k], [source(net, dyn_offset(k), o) for o in LEAF_A])
-            return 0
-
-        lax.fori_loop(0, 7, unit_a, 0)
-
-    for net in range(2):
-        def unit_b(k, _):
-            take(kfb.at[0, k, pl.ds(2, 3)] if net == 0 else kfb.at[1, k], r_b.at[net, k])
-            attend(kfb.at[net, k], [source(net, dyn_offset(k), o) for o in LEAF_B])
-            return 0
-
-        lax.fori_loop(0, 7, unit_b, 0)
+            for cover in covers[hop, j]:
+                cover()
 
     for q in range(n_q):
-        out_ref[q] = (acc[:, pl.ds(q * rows_q, rows_q)] / tot[q]).T.astype(out_ref.dtype)
+        out_ref[q] = (acc[q, pl.ds(0, channels), :] / acc[q, pl.ds(channels, 1), :]).T.astype(out_ref.dtype)
 
     drain(spine, s_spine)
     for j in range(3):
@@ -296,14 +335,18 @@
         return pltpu.VMEM((*lead, half, channels), target.dtype)
 
     dma = pltpu.SemaphoreType.DMA
-    n_q = query_tiles.shape[0]
+    n_q, widest = query_tiles.shape[0], len(LEAF_B)
     scratch = [
         tile(2, 3, 3), tile(3, 7, 3), tile(7, 4), halves(8, 2), tile(7, 2), tile(7, 2), halves(8, 2), tile(28),
         tile(2, 7, 3), tile(2, 7, 5), tile(2, 8),
         pltpu.VMEM((5, 8, n_band), jnp.int32), pltpu.SMEM((6, 8, n_band), jnp.int32),
-        pltpu.VMEM((channels, n_q * rows_q), target.dtype),
-        pltpu.VMEM((channels, n_q * rows_q), jnp.float32),
-        pltpu.VMEM((n_q, 1, rows_q), jnp.float32), pltpu.VMEM((n_q, 1, rows_q), jnp.float32),
+        pltpu.VMEM((n_q, 2 * channels, rows_q), target.dtype),
+        pltpu.VMEM((n_q, channels + 16, rows_q), jnp.float32),
+        pltpu.VMEM((n_q, 1, rows_q), jnp.float32),
+        pltpu.VMEM((channels + 16, widest * rows_q), target.dtype),
+        *[pltpu.VMEM((widest * rows_q, rows_q), jnp.float32)] * 3,
+        *[pltpu.VMEM((widest * rows_q, rows_q), target.dtype)] * 3,
+        *[pltpu.VMEM((widest, 1, rows_q), jnp.float32)] * 3,
         dma, dma((2, 3, 3)), dma((3,)), dma((3, 8, 3)), dma, dma, dma, dma, dma, dma,
         dma((2, 7)), dma((2, 7)), dma((2,)), dma, dma, dma((2,)),
     ]

time: 155 us -> 102 us (0.66)
  Pallas kernels: 149 us -> 96.9 us
    pallas_call x1, Pallas kernels: 149 us -> 96.9 us  [body(): pl.pallas_call(functools.partial(kernel, side), out_shape=jax.ShapeDtypeS...]
where the time goes in v2:
time: 102 us
  Pallas kernels  96.9 us (95%)
  other arithmetic  2.43 us (2%)
  local copies, waits for them, and re-layouts  2.22 us (2%)
    pallas_call x1, Pallas kernels, body(): pl.pallas_call(functools.partial(kernel, side), out_shape=jax.ShapeDtypeS...  96.9 us

profile of v2, /device:TPU:513, one launch (start us, length us, event | category | flops | bytes accessed | tf_op | source)
XLA Modules:
  0.0 101.5 jit_solution(2461776838612949392)
XLA Ops:
  0.0 0.0 copy-start
  0.0 0.7 broadcast_compare_fusion
  0.7 0.0 copy-done
  0.7 0.9 select_reduce_fusion
  1.6 0.1 iota_compare_fusion.1
  1.8 0.1 select_reduce_fusion.1
  1.9 0.6 broadcast_select_fusion.bias_ref
  2.5 0.6 broadcast_in_dim.49.sel_ref
  3.0 96.9 %shard_map.55 = bf16[3,256,128]{2,1,0:T(8,128)(2,1)} custom-call(f32[3,128]{1,0:T(4,128)} %broadcast_select_fusion.bias_ref, s32[8,128]{1,0:T(8,128)} %broadcast_in_dim.49.sel_ref, bf16[3,256,128]{2,1,0:T(8,128)(2,1)} %q_ref.1, bf16[3,256,128]{2,1,0:T(8,128)(2,1)} %own_ref.1), custom_call_target="tpu_custom_call" | custom-call | tf_op jit(solution)/shard_map/pallas_call | solution.py:354
  99.9 1.6 %copy.7 = bf16[3,256,128]{2,1,0:T(8,128)(2,1)} copy(bf16[3,256,128]{2,1,0:T(8,128)(2,1)} %shard_map.55) | data formatting | bytes 393216
  (2 shorter events, 0.0 us)
Async XLA Ops:
  0.0 0.7 copy-start

commit v3 on v2

--- a/solution.py
+++ b/solution.py
@@ -13,7 +13,12 @@
 HEAD = (0, -3, 3)
 LEAF_B = (-3, 3, 2, -2, 4)
 LEAF_A = (0, -1, 1)
-LEAF_G = (0, -1, -2, -3, 1, 2, 3, 4)
+LEAF_G = (0, -1, 1, -2, 2, -3, 3, 4)
+NEAR = 5
+COVERS = {
+    (0, 3): ("near",), (1, 1): ("a1",), (2, 1): ("far",), (1, 2): ("a2",), (2, 2): ("a3",),
+    (1, 3): ("a4", "b1"), (2, 3): ("b2",), (2, 4): ("b3", "b4"),
+}
 
 
 def ring_slot(way, hop):
@@ -24,9 +29,14 @@
     return -(k + 1) if k < 3 else (k - 2 if k < 6 else 4)
 
 
-def kernel(side, bias_ref, sel_ref, q_ref, own_ref, out_ref, *scratch):
-    (spine, row, st_a, st_b1u, st_b1d, st_b2u, st_b2d, st_p, kfa, kfb, kfg, tabv, tabs, qt, acc, mx, ktb,
-     sc0, sc1, sc2, pr0, pr1, pr2, tp0, tp1, tp2, s_spine, r_spine, s_row, r_row, s_a, s_b1u, s_b1d, s_b2u, s_b2d, s_p, r_a, r_b, r_g, s_tab, r_tab, l_tab) = scratch
+def kernel(side, home_ref, cand_ref, valid_ref, q_any, own_any, out_ref, *scratch):
+    (q_ref, own_ref, spine, row, st_a, st_b1u, st_b1d, st_b2u, st_b2d, st_p, kfa, kfb, kfg, table, tabv, tabs, qt, acc,
+     mx, ktb, sc0, sc1, pr0, pr1, tp0, tp1, s_spine, r_spine, s_row, r_row, s_a, s_b1u, s_b1d, s_b2u, s_b2d, s_p,
+     r_a, r_b, r_g, s_tab, r_tab, l_tab) = scratch
+    load_own = pltpu.make_async_copy(own_any, own_ref, l_tab.at[2])
+    load_q = pltpu.make_async_copy(q_any, q_ref, l_tab.at[3])
+    load_own.start()
+    load_q.start()
     n_q, rows_q, channels = q_ref.shape
     half = rows_q // 2
     scale = math.log2(math.e) / math.sqrt(channels)
@@ -97,18 +107,32 @@
         else:
             take(ref, r_row.at[j, ring_slot(way, hop), t])
 
-    send(sel_ref, tabv.at[0], s_tab, r_tab, dev(0, -1))
-    send(sel_ref, tabv.at[1], s_tab, r_tab, dev(0, 1))
-    send(sel_ref, tabv.at[2], s_tab, r_tab, dev(-1, 0, True))
-    send(sel_ref, tabv.at[3], s_tab, r_tab, dev(1, 0, True))
-    send(sel_ref, tabv.at[4], s_tab, r_tab, partner)
+    load_own.wait()
     for t in range(3):
         for way in range(2):
             spine_send(way, 1, t)
             row_send(0, way, 1, t)
-    own_tab = pltpu.make_async_copy(sel_ref, tabs.at[5], l_tab.at[0])
-    own_tab.start()
-
+
+    n_band = table.shape[1]
+    lane = lax.broadcasted_iota(jnp.int32, (1, n_band), 1)
+
+    def fold(k, rows):
+        rows = list(rows)
+        for q in range(n_q):
+            stored = home_ref[cand_ref[q, k]]
+            who = lax.div(stored, own_ref.shape[0])
+            hit = lane == who
+            if q < 2:
+                rows[0] = jnp.where(hit, stored - who * own_ref.shape[0], rows[0])
+                rows[4] = jnp.where(hit, q, rows[4])
+            rows[1 + q] = jnp.where(hit, valid_ref[q, k], rows[1 + q])
+        return tuple(rows)
+
+    blank = jnp.zeros((1, n_band), jnp.int32)
+    built = lax.fori_loop(0, cand_ref.shape[1], fold, (blank,) * 5, unroll=8)
+    for r in range(5):
+        table[pl.ds(r, 1), :] = built[r]
+    load_q.wait()
     for q in range(n_q):
         scaled = q_ref[q].astype(jnp.float32).T * scale
         hi = scaled.astype(qt.dtype)
@@ -116,8 +140,14 @@
         qt[q, pl.ds(channels, channels), :] = (scaled - hi.astype(jnp.float32)).astype(qt.dtype)
     acc[...] = jnp.zeros_like(acc)
     mx[...] = jnp.full_like(mx, NEG)
-    ktb[pl.ds(channels, 16), :] = jnp.ones((16, ktb.shape[1]), ktb.dtype)
-
+
+    send(table, tabv.at[0], s_tab, r_tab, dev(0, -1))
+    send(table, tabv.at[1], s_tab, r_tab, dev(0, 1))
+    send(table, tabv.at[2], s_tab, r_tab, dev(-1, 0, True))
+    send(table, tabv.at[3], s_tab, r_tab, dev(1, 0, True))
+    send(table, tabv.at[4], s_tab, r_tab, partner)
+    own_tab = pltpu.make_async_copy(table, tabs.at[5], l_tab.at[0])
+    own_tab.start()
     own_tab.wait()
     take(tabv, r_tab)
     got = pltpu.make_async_copy(tabv, tabs.at[pl.ds(0, 5)], l_tab.at[1])
@@ -168,73 +198,88 @@
             pack_trunk(row.at[j, k], who, kfb.at[0, k, j - 1], 7 + 7 * j + k, kfb.at[1, k, j - 1], r_b.at[1, k], more)
 
     def pack_spine(way, hop):
-        slot = 3 * way + hop
+        slot = 2 * hop - 1 + way
         more = []
         if hop == 3:
             for o in range(2):
                 if way == 0:
-                    more.append((2 * o, st_b1u.at[7, o], low, kfg.at[o, 7, pl.ds(0, half)], s_b1u, r_g.at[o], up[o]))
+                    more.append((2 * o, st_b1u.at[7, o], low, kfg.at[o, 7, pl.ds(0, half)], s_b1u, r_g.at[2 * o], up[o]))
                 else:
-                    more.append((2 * o + 1, st_b2d.at[7, o], high, kfg.at[o, 7, pl.ds(half, half)], s_b2d, r_g.at[o], down[o]))
-        pack_trunk(spine.at[way, hop - 1], source(0, 0, LEAF_G[slot]), kfg.at[0, slot], slot, kfg.at[1, slot], r_g.at[1], more)
+                    more.append((2 * o + 1, st_b2d.at[7, o], high, kfg.at[o, 7, pl.ds(half, half)], s_b2d, r_g.at[2 * o], down[o]))
+        pack_trunk(spine.at[way, hop - 1], source(0, 0, LEAF_G[slot]), kfg.at[0, slot], slot, kfg.at[1, slot], r_g.at[1 if slot < NEAR else 2], more)
 
     pack_trunk(own_ref, me, kfg.at[0, 0], 0, kfg.at[1, 0], r_g.at[1], [])
 
-    scores, probs, tops = (sc0, sc1, sc2), (pr0, pr1, pr2), (tp0, tp1, tp2)
+    scores, probs, tops = (sc0, sc1), (pr0, pr1), (tp0, tp1)
+    ext = channels + 16
 
     def attend(units, width, ref_of, whos_of):
         keys = width * rows_q
 
-        def score(q, ref):
+        def score(v, ref, whos):
             for t in range(width):
                 k = ref[t]
-                s = jnp.dot(jnp.concatenate([k, k], axis=1), qt[q], preferred_element_type=jnp.float32)
-                scores[q][pl.ds(t * rows_q, rows_q), :] = s
-                tops[q][t] = jnp.max(s, axis=0, keepdims=True)
-
-        def soften(q, bias):
-            before = mx[q]
-            now = before
-            top = [tops[q][t] for t in range(width)]
-            for t in range(width):
-                now = jnp.maximum(now, top[t] + bias[t])
-            for t in range(width):
-                rows = pl.ds(t * rows_q, rows_q)
-                shift = jnp.maximum(now - bias[t], top[t])
-                probs[q][rows, :] = jnp.exp2(scores[q][rows, :] - shift).astype(jnp.bfloat16)
-            mx[q] = now
-            return jnp.exp2(before - now)
-
-        def mix(q, alpha):
-            pv = jnp.dot(ktb[:, pl.ds(0, keys)], probs[q][pl.ds(0, keys), :], preferred_element_type=jnp.float32)
-            acc[q] = acc[q] * alpha + pv
+                rhs = qt[2] if v == 1 else qt[tabs[5, 4, whos[t]]]
+                s = jnp.dot(jnp.concatenate([k, k], axis=1), rhs, preferred_element_type=jnp.float32)
+                scores[v][pl.ds(t * rows_q, rows_q), :] = s
+                tops[v][t] = jnp.max(s, axis=0, keepdims=True)
+
+        def soften(v, t, shift):
+            rows = pl.ds(t * rows_q, rows_q)
+            probs[v][rows, :] = jnp.exp2(scores[v][rows, :] - shift).astype(jnp.bfloat16)
+
+        def bias(q, who):
+            return jnp.where(tabs[5, 1 + q, who] > 0, 0.0, NEG).astype(jnp.float32)
 
         def unit(u, _):
-            ref = ref_of(u)
-            following = ref_of(jnp.minimum(u + 1, units - 1))
-            whos = whos_of(u)
-            ktb[pl.ds(0, channels), pl.ds(0, keys)] = ref[...].reshape(keys, channels).T
-            alphas = []
-            for q in range(n_q):
-                score((q + 1) % n_q, ref if q + 1 < n_q else following)
-                alphas.append(soften(q, [bias_ref[q, who] for who in whos]))
-                if q > 0:
-                    mix(q - 1, alphas[q - 1])
-            mix(n_q - 1, alphas[n_q - 1])
+            ref, whos = ref_of(u), whos_of(u)
+            later = jnp.minimum(u + 1, units - 1)
+            second = [tabs[5, 4, who] == 1 for who in whos]
+            b = [[bias(q, who) for who in whos] for q in range(3)]
+            for t in range(width):
+                kt = jnp.concatenate([ref[t].T, jnp.ones((16, rows_q), jnp.bfloat16)], axis=0)
+                none = jnp.zeros_like(kt)
+                cols = pl.ds(t * rows_q, rows_q)
+                ktb[pl.ds(0, ext), cols] = jnp.where(second[t], none, kt)
+                ktb[pl.ds(ext, ext), cols] = jnp.where(second[t], kt, none)
+                ktb[pl.ds(2 * ext, ext), cols] = kt
+            score(1, ref, whos)
+            before = [mx[q] for q in range(3)]
+            now = list(before)
+            for t in range(width):
+                for q in range(2):
+                    now[q] = jnp.maximum(now[q], tops[0][t] + b[q][t])
+            for t in range(width):
+                base = jnp.where(second[t], now[1], now[0]) - jnp.maximum(b[0][t], b[1][t])
+                soften(0, t, jnp.maximum(base, tops[0][t]))
+            pv = jnp.dot(ktb[pl.ds(0, 2 * ext), pl.ds(0, keys)], probs[0][pl.ds(0, keys), :],
+                         preferred_element_type=jnp.float32)
+            for q in range(2):
+                acc[q] = acc[q] * jnp.exp2(before[q] - now[q]) + pv[q * ext:(q + 1) * ext]
+            score(0, ref_of(later), whos_of(later))
+            for t in range(width):
+                now[2] = jnp.maximum(now[2], tops[1][t] + b[2][t])
+            for t in range(width):
+                soften(1, t, jnp.maximum(now[2] - b[2][t], tops[1][t]))
+            pv = jnp.dot(ktb[pl.ds(2 * ext, ext), pl.ds(0, keys)], probs[1][pl.ds(0, keys), :],
+                         preferred_element_type=jnp.float32)
+            acc[2] = acc[2] * jnp.exp2(before[2] - now[2]) + pv
+            for q in range(3):
+                mx[q] = now[q]
             return 0
 
-        score(0, ref_of(0))
+        score(0, ref_of(0), whos_of(0))
         lax.fori_loop(0, units, unit, 0)
 
-    def attend_g():
+    def attend_near():
+        take(kfg.at[1, pl.ds(0, NEAR)], r_g.at[1])
+        attend(2, NEAR, lambda u: kfg.at[u, pl.ds(0, NEAR)], lambda u: [source(u, 0, o) for o in LEAF_G[:NEAR]])
+
+    def attend_far():
+        far = len(LEAF_G) - NEAR
         take(kfg.at[0, 7], r_g.at[0])
-        take(kfg.at[1], r_g.at[1])
-
-        def whos(u):
-            offs = [jnp.where(lax.rem(u, 2) == 0, LEAF_G[t], LEAF_G[4 + t]) for t in range(4)]
-            return [source(lax.div(u, 2), 0, o) for o in offs]
-
-        attend(4, 4, lambda u: kfg.at[lax.div(u, 2), pl.ds(4 * lax.rem(u, 2), 4)], whos)
+        take(kfg.at[1, pl.ds(NEAR, far)], r_g.at[2])
+        attend(2, far, lambda u: kfg.at[u, pl.ds(NEAR, far)], lambda u: [source(u, 0, o) for o in LEAF_G[NEAR:]])
 
     def attend_row(hop, ref, sem, skip, offs):
         ways = 2 if hop < 4 else 1
@@ -257,11 +302,19 @@
 
         attend(2 * ways, len(offs), unit_ref, whos)
 
-    def attend_a(hop):
-        attend_row(hop, kfa, r_a, 1, LEAF_A)
-
-    def attend_b(hop):
-        attend_row(hop, kfb, r_b, 2, LEAF_B)
+    def cover(name):
+        if name == "near":
+            attend_near()
+        elif name == "far":
+            attend_far()
+        elif name[0] == "a":
+            attend_row(int(name[1]), kfa, r_a, 1, LEAF_A)
+        else:
+            attend_row(int(name[1]), kfb, r_b, 2, LEAF_B)
+
+    def covers(step):
+        for name in COVERS.get(step, ()):
+            cover(name)
 
     for hop in range(1, 4):
         for t in range(3):
@@ -279,16 +332,12 @@
         for way in range(2):
             pack_row(0, ring_slot(way, hop))
             pack_spine(way, hop)
+        covers((0, hop))
     for t in range(3):
         for way in range(2):
             row_take(0, way, 4, t)
     pack_row(0, 6)
-    covers = {
-        (1, 1): [attend_g], (1, 2): [lambda: attend_a(1)],
-        (2, 1): [lambda: attend_a(2)], (2, 2): [lambda: attend_a(3)],
-        (3, 1): [lambda: attend_a(4)], (3, 2): [lambda: attend_b(1)],
-        (4, 1): [], (4, 2): [lambda: attend_b(2), lambda: attend_b(3), lambda: attend_b(4)],
-    }
+    covers((0, 4))
     for hop in range(1, 5):
         for j in (1, 2):
             for t in range(3):
@@ -298,8 +347,7 @@
                         row_send(j, way, hop + 1, t)
             for way in range(2 if hop < 4 else 1):
                 pack_row(j, ring_slot(way, hop))
-            for cover in covers[hop, j]:
-                cover()
+            covers((j, hop))
 
     for q in range(n_q):
         out_ref[q] = (acc[q, pl.ds(0, channels), :] / acc[q, pl.ds(channels, 1), :]).T.astype(out_ref.dtype)
@@ -320,13 +368,6 @@
     n_band = 2 * side * side
     tiles_dev, rows_q, channels = target.shape
     half = rows_q // 2
-    ids = lax.broadcasted_iota(jnp.int32, (1, 1, tile_home.shape[0]), 2)
-    stored = jnp.sum(jnp.where(candidates[:, :, None] == ids, tile_home[None, None, :], 0), axis=2)
-    hit = (stored // tiles_dev)[:, :, None] == lax.broadcasted_iota(jnp.int32, (1, 1, n_band), 2)
-    sel = jnp.sum(jnp.where(hit[:2], (stored % tiles_dev)[:2, :, None], 0), axis=(0, 1))
-    sel = jnp.broadcast_to(sel[None, :], (8, n_band))
-    used = jnp.any(hit & (valid_mask > 0)[:, :, None], axis=1)
-    bias = jnp.where(used, 0.0, NEG).astype(jnp.float32)
 
     def tile(*lead):
         return pltpu.VMEM((*lead, rows_q, channels), target.dtype)
@@ -337,30 +378,31 @@
     dma = pltpu.SemaphoreType.DMA
     n_q, widest = query_tiles.shape[0], len(LEAF_B)
     scratch = [
-        tile(2, 3, 3), tile(3, 7, 3), tile(7, 4), halves(8, 2), tile(7, 2), tile(7, 2), halves(8, 2), tile(28),
+        tile(n_q), tile(tiles_dev), tile(2, 3, 3), tile(3, 7, 3), tile(7, 4), halves(8, 2), tile(7, 2), tile(7, 2), halves(8, 2), tile(28),
         tile(2, 7, 3), tile(2, 7, 5), tile(2, 8),
-        pltpu.VMEM((5, 8, n_band), jnp.int32), pltpu.SMEM((6, 8, n_band), jnp.int32),
+        pltpu.VMEM((8, n_band), jnp.int32), pltpu.VMEM((5, 8, n_band), jnp.int32), pltpu.SMEM((6, 8, n_band), jnp.int32),
         pltpu.VMEM((n_q, 2 * channels, rows_q), target.dtype),
         pltpu.VMEM((n_q, channels + 16, rows_q), jnp.float32),
         pltpu.VMEM((n_q, 1, rows_q), jnp.float32),
-        pltpu.VMEM((channels + 16, widest * rows_q), target.dtype),
-        *[pltpu.VMEM((widest * rows_q, rows_q), jnp.float32)] * 3,
-        *[pltpu.VMEM((widest * rows_q, rows_q), target.dtype)] * 3,
-        *[pltpu.VMEM((widest, 1, rows_q), jnp.float32)] * 3,
+        pltpu.VMEM((3 * (channels + 16), widest * rows_q), target.dtype),
+        *[pltpu.VMEM((widest * rows_q, rows_q), jnp.float32)] * 2,
+        *[pltpu.VMEM((widest * rows_q, rows_q), target.dtype)] * 2,
+        *[pltpu.VMEM((widest, 1, rows_q), jnp.float32)] * 2,
         dma, dma((2, 3, 3)), dma((3,)), dma((3, 8, 3)), dma, dma, dma, dma, dma, dma,
-        dma((2, 7)), dma((2, 7)), dma((2,)), dma, dma, dma((2,)),
+        dma((2, 7)), dma((2, 7)), dma((3,)), dma, dma, dma((4,)),
     ]
-    vmem = pl.BlockSpec(memory_space=pltpu.VMEM)
+    smem = pl.BlockSpec(memory_space=pltpu.SMEM)
+    anywhere = pl.BlockSpec(memory_space=pl.ANY)
     return pl.pallas_call(
         functools.partial(kernel, side),
         out_shape=jax.ShapeDtypeStruct(query_tiles.shape, query_tiles.dtype),
-        in_specs=[pl.BlockSpec(memory_space=pltpu.SMEM), vmem, vmem, vmem],
-        out_specs=vmem,
+        in_specs=[smem, smem, smem, anywhere, anywhere],
+        out_specs=pl.BlockSpec(memory_space=pltpu.VMEM),
         scratch_shapes=scratch,
         compiler_params=pltpu.CompilerParams(
             collective_id=0, has_side_effects=True, vmem_limit_bytes=60 * 1024 * 1024
         ),
-    )(bias, sel, query_tiles, target)
+    )(tile_home, candidates, valid_mask, query_tiles, target)
 
 
 def solution(mesh):

time: 102 us -> 96.4 us (0.945)
  other arithmetic: 2.43 us -> 0 us
  Pallas kernels: 96.9 us -> 94.6 us
    pallas_call x1, Pallas kernels: 96.9 us -> 94.6 us  [body(): pl.pallas_call(functools.partial(kernel, side), out_shape=jax.ShapeDtypeS...]
where the time goes in v3:
time: 96.4 us; the launch traced here: 96.2 us
  Pallas kernels  94.6 us (98%)
  local copies, waits for them, and re-layouts  1.62 us (2%)
    pallas_call x1, Pallas kernels, body(): pl.pallas_call(functools.partial(kernel, side), out_shape=jax.ShapeDtypeS...  94.6 us

profile of v3, /device:TPU:513, one launch (start us, length us, event | category | flops | bytes accessed | tf_op | source)
XLA Modules:
  0.0 96.2 jit_solution(1830777224971056319)
XLA Ops:
  0.0 94.6 %shard_map.55 = bf16[3,256,128]{2,1,0:T(8,128)(2,1)} custom-call(s32[384]{0:T(512)} %home_ref.1, s32[3,64]{1,0:T(4,128)} %cand_ref.1, s32[3,64]{1,0:T(4,128)} %valid_ref.1, bf16[3,256,128]{2,1,0:T(8,128)(2,1)} %q_any.1, bf16[3,256,128]{2,1,0:T(8,128)(2,1)} %own_any.1), custom_call_target="tpu_custom_call" | custom-call | tf_op jit(solution)/shard_map/pallas_call | solution.py:396
  94.6 1.6 %copy.7 = bf16[3,256,128]{2,1,0:T(8,128)(2,1)} copy(bf16[3,256,128]{2,1,0:T(8,128)(2,1)} %shard_map.55) | data formatting | bytes 393216

commit v4 on v3

--- a/solution.py
+++ b/solution.py
@@ -15,10 +15,11 @@
 LEAF_A = (0, -1, 1)
 LEAF_G = (0, -1, 1, -2, 2, -3, 3, 4)
 NEAR = 5
-COVERS = {
-    (0, 3): ("near",), (1, 1): ("a1",), (2, 1): ("far",), (1, 2): ("a2",), (2, 2): ("a3",),
-    (1, 3): ("a4", "b1"), (2, 3): ("b2",), (2, 4): ("b3", "b4"),
-}
+PLAN = (
+    "s1", "init", "r01", "s2", "own", "z1", "s3", "z3", "r02", "z2", "r21", "r11", "p01", "r03", "p21",
+    "near", "r22", "p11", "p22", "far", "r12", "p12", "p03", "a1", "p02", "b1", "r04", "r23", "p04", "p23",
+    "r13", "p13", "b2", "a3", "r24", "r14", "a2", "p24", "p14", "a4", "b3", "b4",
+)
 
 
 def ring_slot(way, hop):
@@ -29,14 +30,18 @@
     return -(k + 1) if k < 3 else (k - 2 if k < 6 else 4)
 
 
-def kernel(side, home_ref, cand_ref, valid_ref, q_any, own_any, out_ref, *scratch):
-    (q_ref, own_ref, spine, row, st_a, st_b1u, st_b1d, st_b2u, st_b2d, st_p, kfa, kfb, kfg, table, tabv, tabs, qt, acc,
+def kernel(side, home_any, cand_any, valid_any, q_any, own_any, out_ref, *scratch):
+    (home_ref, cand_ref, valid_ref, q_ref, own_ref, spine, row, st_a, st_b1u, st_b1d, st_b2u, st_b2d, st_p, kfa, kfb, kfg, table, tabv, tabs, qt, acc,
      mx, ktb, sc0, sc1, pr0, pr1, tp0, tp1, s_spine, r_spine, s_row, r_row, s_a, s_b1u, s_b1d, s_b2u, s_b2d, s_p,
      r_a, r_b, r_g, s_tab, r_tab, l_tab) = scratch
     load_own = pltpu.make_async_copy(own_any, own_ref, l_tab.at[2])
     load_q = pltpu.make_async_copy(q_any, q_ref, l_tab.at[3])
-    load_own.start()
-    load_q.start()
+    load_tables = [
+        pltpu.make_async_copy(src, dst, l_tab.at[4 + i])
+        for i, (src, dst) in enumerate(((home_any, home_ref), (cand_any, cand_ref), (valid_any, valid_ref)))
+    ]
+    for load in (*load_tables, load_own, load_q):
+        load.start()
     n_q, rows_q, channels = q_ref.shape
     half = rows_q // 2
     scale = math.log2(math.e) / math.sqrt(channels)
@@ -82,36 +87,6 @@
             greeted += [dev(d, 0, other), dev(0, d, other)]
     for to in greeted:
         pl.semaphore_signal(barrier, inc=1, device_id=to, device_id_type=MESH)
-    pl.semaphore_wait(barrier, len(greeted))
-
-    def head(j):
-        return own_ref if j == 0 else spine.at[j - 1, 2]
-
-    def spine_send(way, hop, t):
-        src = own_ref.at[t] if hop == 1 else spine.at[way, hop - 2, t]
-        send(src, spine.at[way, hop - 1, t], s_spine, r_spine.at[way, hop - 1, t], dev(0, 1 - 2 * way))
-
-    def row_send(j, way, hop, t):
-        src = head(j).at[t] if hop == 1 else row.at[j, ring_slot(way, hop - 1), t]
-        dst = row.at[j, ring_slot(way, hop), t]
-        sem = r_row.at[j, ring_slot(way, hop), t]
-        if hop == 4:
-            part = pl.ds(way * half, half)
-            src, dst, sem = src.at[part], dst.at[part], r_row.at[j, 6 + way, t]
-        send(src, dst, s_row.at[j], sem, dev(1 - 2 * way, 0))
-
-    def row_take(j, way, hop, t):
-        ref = row.at[j, ring_slot(way, hop), t]
-        if hop == 4:
-            take(ref.at[pl.ds(way * half, half)], r_row.at[j, 6 + way, t])
-        else:
-            take(ref, r_row.at[j, ring_slot(way, hop), t])
-
-    load_own.wait()
-    for t in range(3):
-        for way in range(2):
-            spine_send(way, 1, t)
-            row_send(0, way, 1, t)
 
     n_band = table.shape[1]
     lane = lax.broadcasted_iota(jnp.int32, (1, n_band), 1)
@@ -128,18 +103,42 @@
             rows[1 + q] = jnp.where(hit, valid_ref[q, k], rows[1 + q])
         return tuple(rows)
 
+    for load in load_tables:
+        load.wait()
     blank = jnp.zeros((1, n_band), jnp.int32)
     built = lax.fori_loop(0, cand_ref.shape[1], fold, (blank,) * 5, unroll=8)
     for r in range(5):
         table[pl.ds(r, 1), :] = built[r]
-    load_q.wait()
-    for q in range(n_q):
-        scaled = q_ref[q].astype(jnp.float32).T * scale
-        hi = scaled.astype(qt.dtype)
-        qt[q, pl.ds(0, channels), :] = hi
-        qt[q, pl.ds(channels, channels), :] = (scaled - hi.astype(jnp.float32)).astype(qt.dtype)
-    acc[...] = jnp.zeros_like(acc)
-    mx[...] = jnp.full_like(mx, NEG)
+    pl.semaphore_wait(barrier, len(greeted))
+
+    def head(j):
+        return own_ref if j == 0 else spine.at[j - 1, 2]
+
+    def spine_send(way, hop, t):
+        src = own_ref.at[t] if hop == 1 else spine.at[way, hop - 2, t]
+        send(src, spine.at[way, hop - 1, t], s_spine, r_spine.at[way, hop - 1, t], dev(0, 1 - 2 * way))
+
+    def row_send(j, way, hop, t):
+        src = head(j).at[t] if hop == 1 else row.at[j, ring_slot(way, hop - 1), t]
+        dst = row.at[j, ring_slot(way, hop), t]
+        sem = r_row.at[j, ring_slot(way, hop), t]
+        if hop == 4:
+            part = pl.ds(way * half, half)
+            src, dst, sem = src.at[part], dst.at[part], r_row.at[j, 6 + way, t]
+        send(src, dst, s_row.at[j], sem, dev(1 - 2 * way, 0))
+
+    def row_take(j, way, hop, t):
+        ref = row.at[j, ring_slot(way, hop), t]
+        if hop == 4:
+            take(ref.at[pl.ds(way * half, half)], r_row.at[j, 6 + way, t])
+        else:
+            take(ref, r_row.at[j, ring_slot(way, hop), t])
+
+    load_own.wait()
+    for t in range(3):
+        for way in range(2):
+            spine_send(way, 1, t)
+            row_send(0, way, 1, t)
 
     send(table, tabv.at[0], s_tab, r_tab, dev(0, -1))
     send(table, tabv.at[1], s_tab, r_tab, dev(0, 1))
@@ -148,11 +147,24 @@
     send(table, tabv.at[4], s_tab, r_tab, partner)
     own_tab = pltpu.make_async_copy(table, tabs.at[5], l_tab.at[0])
     own_tab.start()
-    own_tab.wait()
-    take(tabv, r_tab)
-    got = pltpu.make_async_copy(tabv, tabs.at[pl.ds(0, 5)], l_tab.at[1])
-    got.start()
-    got.wait()
+
+    def init():
+        load_q.wait()
+        for q in range(n_q):
+            scaled = q_ref[q].astype(jnp.float32).T * scale
+            hi = scaled.astype(qt.dtype)
+            qt[q, pl.ds(0, channels), :] = hi
+            qt[q, pl.ds(channels, channels), :] = (scaled - hi.astype(jnp.float32)).astype(qt.dtype)
+        acc[...] = jnp.zeros_like(acc)
+        mx[...] = jnp.full_like(mx, NEG)
+
+    def own():
+        own_tab.wait()
+        take(tabv, r_tab)
+        got = pltpu.make_async_copy(tabv, tabs.at[pl.ds(0, 5)], l_tab.at[1])
+        got.start()
+        got.wait()
+        pack_trunk(own_ref, me, kfg.at[0, 0], 0, kfg.at[1, 0], r_g.at[1], [])
 
     def pack(src, who, outs):
         step = 64
@@ -208,8 +220,6 @@
                     more.append((2 * o + 1, st_b2d.at[7, o], high, kfg.at[o, 7, pl.ds(half, half)], s_b2d, r_g.at[2 * o], down[o]))
         pack_trunk(spine.at[way, hop - 1], source(0, 0, LEAF_G[slot]), kfg.at[0, slot], slot, kfg.at[1, slot], r_g.at[1 if slot < NEAR else 2], more)
 
-    pack_trunk(own_ref, me, kfg.at[0, 0], 0, kfg.at[1, 0], r_g.at[1], [])
-
     scores, probs, tops = (sc0, sc1), (pr0, pr1), (tp0, tp1)
     ext = channels + 16
 
@@ -302,21 +312,7 @@
 
         attend(2 * ways, len(offs), unit_ref, whos)
 
-    def cover(name):
-        if name == "near":
-            attend_near()
-        elif name == "far":
-            attend_far()
-        elif name[0] == "a":
-            attend_row(int(name[1]), kfa, r_a, 1, LEAF_A)
-        else:
-            attend_row(int(name[1]), kfb, r_b, 2, LEAF_B)
-
-    def covers(step):
-        for name in COVERS.get(step, ()):
-            cover(name)
-
-    for hop in range(1, 4):
+    def spine_step(hop):
         for t in range(3):
             for way in range(2):
                 take(spine.at[way, hop - 1, t], r_spine.at[way, hop - 1, t])
@@ -325,29 +321,38 @@
                 else:
                     for w in range(2):
                         row_send(1 + way, w, 1, t)
+
+    def row_step(j, hop):
         for t in range(3):
             for way in range(2):
-                row_take(0, way, hop, t)
-                row_send(0, way, hop + 1, t)
-        for way in range(2):
-            pack_row(0, ring_slot(way, hop))
-            pack_spine(way, hop)
-        covers((0, hop))
-    for t in range(3):
-        for way in range(2):
-            row_take(0, way, 4, t)
-    pack_row(0, 6)
-    covers((0, 4))
-    for hop in range(1, 5):
-        for j in (1, 2):
-            for t in range(3):
-                for way in range(2):
-                    row_take(j, way, hop, t)
-                    if hop < 4:
-                        row_send(j, way, hop + 1, t)
-            for way in range(2 if hop < 4 else 1):
-                pack_row(j, ring_slot(way, hop))
-            covers((j, hop))
+                row_take(j, way, hop, t)
+                if hop < 4:
+                    row_send(j, way, hop + 1, t)
+
+    for step in PLAN:
+        kind, hop = step[0], step[-1]
+        if step == "init":
+            init()
+        elif step == "own":
+            own()
+        elif step == "near":
+            attend_near()
+        elif step == "far":
+            attend_far()
+        elif kind == "s":
+            spine_step(int(hop))
+        elif kind == "r":
+            row_step(int(step[1]), int(hop))
+        elif kind == "z":
+            for way in range(2):
+                pack_spine(way, int(hop))
+        elif kind == "p":
+            for way in range(2 if hop < "4" else 1):
+                pack_row(int(step[1]), ring_slot(way, int(hop)))
+        elif kind == "a":
+            attend_row(int(hop), kfa, r_a, 1, LEAF_A)
+        else:
+            attend_row(int(hop), kfb, r_b, 2, LEAF_B)
 
     for q in range(n_q):
         out_ref[q] = (acc[q, pl.ds(0, channels), :] / acc[q, pl.ds(channels, 1), :]).T.astype(out_ref.dtype)
@@ -378,6 +383,7 @@
     dma = pltpu.SemaphoreType.DMA
     n_q, widest = query_tiles.shape[0], len(LEAF_B)
     scratch = [
+        *[pltpu.SMEM(a.shape, a.dtype) for a in (tile_home, candidates, valid_mask)],
         tile(n_q), tile(tiles_dev), tile(2, 3, 3), tile(3, 7, 3), tile(7, 4), halves(8, 2), tile(7, 2), tile(7, 2), halves(8, 2), tile(28),
         tile(2, 7, 3), tile(2, 7, 5), tile(2, 8),
         pltpu.VMEM((8, n_band), jnp.int32), pltpu.VMEM((5, 8, n_band), jnp.int32), pltpu.SMEM((6, 8, n_band), jnp.int32),
@@ -389,14 +395,13 @@
         *[pltpu.VMEM((widest * rows_q, rows_q), target.dtype)] * 2,
         *[pltpu.VMEM((widest, 1, rows_q), jnp.float32)] * 2,
         dma, dma((2, 3, 3)), dma((3,)), dma((3, 8, 3)), dma, dma, dma, dma, dma, dma,
-        dma((2, 7)), dma((2, 7)), dma((3,)), dma, dma, dma((4,)),
+        dma((2, 7)), dma((2, 7)), dma((3,)), dma, dma, dma((7,)),
     ]
-    smem = pl.BlockSpec(memory_space=pltpu.SMEM)
-    anywhere = pl.BlockSpec(memory_space=pl.ANY)
+    stored = pl.BlockSpec(memory_space=pltpu.HBM)
     return pl.pallas_call(
         functools.partial(kernel, side),
         out_shape=jax.ShapeDtypeStruct(query_tiles.shape, query_tiles.dtype),
-        in_specs=[smem, smem, smem, anywhere, anywhere],
+        in_specs=[stored] * 5,
         out_specs=pl.BlockSpec(memory_space=pltpu.VMEM),
         scratch_shapes=scratch,
         compiler_params=pltpu.CompilerParams(

time: 96.4 us -> 89.2 us (0.925)
  Pallas kernels: 94.6 us -> 87.4 us
    pallas_call x1, Pallas kernels: 94.6 us -> 87.4 us  [body(): pl.pallas_call(functools.partial(kernel, side), out_shape=jax.ShapeDtypeS...]
where the time goes in v4:
time: 89.2 us; the launch traced here: 89 us
  Pallas kernels  87.4 us (98%)
  local copies, waits for them, and re-layouts  1.62 us (2%)
    pallas_call x1, Pallas kernels, body(): pl.pallas_call(functools.partial(kernel, side), out_shape=jax.ShapeDtypeS...  87.4 us

profile of v4, /device:TPU:513, one launch (start us, length us, event | category | flops | bytes accessed | tf_op | source)
XLA Modules:
  0.0 89.0 jit_solution(10939826860557216848)
XLA Ops:
  0.0 87.4 %shard_map.55 = bf16[3,256,128]{2,1,0:T(8,128)(2,1)} custom-call(s32[384]{0:T(512)} %home_any.1, s32[3,64]{1,0:T(4,128)} %cand_any.1, s32[3,64]{1,0:T(4,128)} %valid_any.1, bf16[3,256,128]{2,1,0:T(8,128)(2,1)} %q_any.1, bf16[3,256,128]{2,1,0:T(8,128)(2,1)} %own_any.1), custom_call_target="tpu_custom_call" | custom-call | tf_op jit(solution)/shard_map/pallas_call | solution.py:401
  87.4 1.6 %copy.7 = bf16[3,256,128]{2,1,0:T(8,128)(2,1)} copy(bf16[3,256,128]{2,1,0:T(8,128)(2,1)} %shard_map.55) | data formatting | bytes 393216

commit v5 on v4

--- a/solution.py
+++ b/solution.py
@@ -262,10 +262,10 @@
             for t in range(width):
                 base = jnp.where(second[t], now[1], now[0]) - jnp.maximum(b[0][t], b[1][t])
                 soften(0, t, jnp.maximum(base, tops[0][t]))
-            pv = jnp.dot(ktb[pl.ds(0, 2 * ext), pl.ds(0, keys)], probs[0][pl.ds(0, keys), :],
-                         preferred_element_type=jnp.float32)
             for q in range(2):
-                acc[q] = acc[q] * jnp.exp2(before[q] - now[q]) + pv[q * ext:(q + 1) * ext]
+                pv = jnp.dot(ktb[pl.ds(q * ext, ext), pl.ds(0, keys)], probs[0][pl.ds(0, keys), :],
+                             preferred_element_type=jnp.float32)
+                acc[q] = acc[q] * jnp.exp2(before[q] - now[q]) + pv
             score(0, ref_of(later), whos_of(later))
             for t in range(width):
                 now[2] = jnp.maximum(now[2], tops[1][t] + b[2][t])

time: 89.2 us -> 87.9 us (0.985)
  Pallas kernels: 87.4 us -> 86.2 us
    pallas_call x1, Pallas kernels: 87.4 us -> 86.2 us  [body(): pl.pallas_call(functools.partial(kernel, side), out_shape=jax.ShapeDtypeS...]
where the time goes in v5:
time: 87.9 us; the launch traced here: 87.8 us
  Pallas kernels  86.2 us (98%)
  local copies, waits for them, and re-layouts  1.62 us (2%)
    pallas_call x1, Pallas kernels, body(): pl.pallas_call(functools.partial(kernel, side), out_shape=jax.ShapeDtypeS...  86.2 us

profile of v5, /device:TPU:513, one launch (start us, length us, event | category | flops | bytes accessed | tf_op | source)
XLA Modules:
  0.0 87.8 jit_solution(5957947295666868280)
XLA Ops:
  0.0 86.2 %shard_map.55 = bf16[3,256,128]{2,1,0:T(8,128)(2,1)} custom-call(s32[384]{0:T(512)} %home_any.1, s32[3,64]{1,0:T(4,128)} %cand_any.1, s32[3,64]{1,0:T(4,128)} %valid_any.1, bf16[3,256,128]{2,1,0:T(8,128)(2,1)} %q_any.1, bf16[3,256,128]{2,1,0:T(8,128)(2,1)} %own_any.1), custom_call_target="tpu_custom_call" | custom-call | tf_op jit(solution)/shard_map/pallas_call | solution.py:401
  86.2 1.6 %copy.7 = bf16[3,256,128]{2,1,0:T(8,128)(2,1)} copy(bf16[3,256,128]{2,1,0:T(8,128)(2,1)} %shard_map.55) | data formatting | bytes 393216
